TPU v7x, 32 devices: a whole 2x2x4 slice. The times are simulated.
32 devices in a mesh: dp: 8 (over z, y), mp: 4 (over x, core).
Axes of the slice: x: 2, y: 2, z: 4, core: 2. Of those that a mesh axis runs over, the one named last changes fastest.
Arguments:
- image_tokens: bfloat16 [8, 192, 3072], P('dp'), may hold values from -6 to 6
- text_tokens: bfloat16 [8, 64, 3072], P('dp'), may hold values from -6 to 6
- null_prompt: bfloat16 [64, 3072], replicated, may hold values from -6 to 6
- drop_flags: int32 [8], P('dp'), may hold values 0 or 1
- time_index: int32 [8], P('dp'), may hold values from 0 to 31
- modulation: float32 [32, 3, 3072], replicated, may hold values from -3 to 3
- w_up: bfloat16 [3072, 12288], P('dp', 'mp'), may hold values from -0.109375 to 0.109375
- w_down: bfloat16 [12288, 3072], P('mp', 'dp'), may hold values from -0.0546875 to 0.0546875
- d_output: bfloat16 [8, 256, 3072], P('dp'), may hold values from -6 to 6
Outputs:
- block_out: bfloat16 [8, 256, 3072], P('dp')
- d_tokens: bfloat16 [8, 256, 3072], P('dp')
- grad_up: float32 [3072, 12288], P('dp', 'mp')
- grad_down: float32 [12288, 3072], P('mp', 'dp')
- grad_null: float32 [64, 3072], replicated
All inputs are finite; a program needn't handle non-finite values. No bound on the sum of `drop_flags` on one device may be relied on, other than what follows from the above.
Results may differ from a plain program's by a relative error of at most 0.017.
Values may be sent and summed in bfloat16 or wider, within the bound.
A program may use at most 128 MiB of HBM per device.

v0:
```python
import functools
import jax
import jax.numpy as jnp
from jax import lax
from jax.sharding import PartitionSpec as P

EPS = 1e-06
BF16 = jnp.bfloat16
F32 = jnp.float32


def gelu_tanh(values):
    return jax.nn.gelu(values, approximate=True)


def dot(left, right, dims):
    return lax.dot_general(left, right, (dims, ((), ())), preferred_element_type=F32)


def swap(values, axis, size, bit):
    return lax.ppermute(values, axis, [(i, i ^ bit) for i in range(size)])


def shards(
    dp,
    mp,
    image_tokens,
    text_tokens,
    null_prompt,
    drop_flags,
    time_index,
    modulation,
    w_up,
    w_down,
    d_output,
):
    lines = [list(range(parity, dp, 2)) for parity in range(2)]
    per_line = dp // 2
    bits = []
    bit = 1
    while bit < mp:
        bits.append(bit)
        bit *= 2
    d_rows, ff_m = w_up.shape
    f = ff_m // dp
    width = d_rows * dp
    up_own = lax.all_to_all(
        w_up.reshape(d_rows, dp, f).transpose(1, 0, 2), "dp", 0, 0, tiled=True
    ).reshape(width, f)
    down_own = (
        lax.all_to_all(w_down.reshape(dp, f, d_rows), "dp", 0, 0, tiled=True)
        .transpose(1, 0, 2)
        .reshape(f, width)
    )
    up_other = swap(up_own, "dp", dp, 1)
    down_other = swap(down_own, "dp", dp, 1)
    m = lax.axis_index("mp")
    n_text = text_tokens.shape[1] // mp
    n_image = image_tokens.shape[1] // mp
    all_text = text_tokens.shape[1]

    def share(text_part, image_part):
        t = lax.dynamic_slice_in_dim(text_part, m * n_text, n_text, 0)
        i = lax.dynamic_slice_in_dim(image_part, m * n_image, n_image, 0)
        return jnp.concatenate([t, i], axis=0)

    dropped = drop_flags[0] == 1
    joined32 = share(jnp.where(dropped, null_prompt, text_tokens[0]), image_tokens[0]).astype(F32)
    d_out32 = share(d_output[0, :all_text], d_output[0, all_text:]).astype(F32)
    level = lax.dynamic_index_in_dim(modulation, time_index[0], 0, keepdims=False)
    shift, scale, gate = (level[0][None], level[1][None], level[2][None])
    centred = joined32 - jnp.mean(joined32, axis=-1, keepdims=True)
    inv_std = lax.rsqrt(jnp.mean(centred * centred, axis=-1, keepdims=True) + EPS)
    normed = centred * inv_std
    mod_in = (normed * (1.0 + scale) + shift).astype(BF16)
    d_branch = (d_out32 * gate).astype(BF16)

    def gather(rows):
        rows = lax.all_gather(rows, "dp", axis=0, tiled=True, axis_index_groups=lines)
        for b in reversed(bits):
            rows = jnp.concatenate([rows, swap(rows, "mp", mp, b)], axis=0)
        return rows

    def scatter(own, other, block_own, block_other, contract):

        def product(rows):
            return dot(own[rows], block_own, contract) + dot(other[rows], block_other, contract)

        half = own.shape[0] // 2
        sent = swap(product(slice(half, None)).astype(BF16), "mp", mp, bits[0])
        total = product(slice(0, half)) + sent.astype(F32)
        for b in bits[1:]:
            half = total.shape[0] // 2
            total = total[:half] + swap(total[half:].astype(BF16), "mp", mp, b).astype(F32)
        parts = lax.all_to_all(
            total.astype(BF16).reshape(per_line, -1, width),
            "dp",
            0,
            0,
            tiled=True,
            axis_index_groups=lines,
        )
        return jnp.sum(parts.astype(F32), axis=0)

    tokens = gather(mod_in)
    d_tok = gather(d_branch)

    def half_block(up, down):
        pre = dot(tokens, up, ((1,), (0,)))
        hid, back = jax.vjp(gelu_tanh, pre)
        d_hid = dot(d_tok, down, ((1,), (1,)))
        return (hid.astype(BF16), back(d_hid)[0].astype(BF16))

    hid_own, dpre_own = half_block(up_own, down_own)
    hid_other, dpre_other = half_block(up_other, down_other)
    branch = scatter(hid_own, hid_other, down_own, down_other, ((1,), (0,)))
    d_mod = scatter(dpre_own, dpre_other, up_own, up_other, ((1,), (1,)))
    up_sent = dot(tokens, dpre_other, ((0,), (0,))).astype(BF16)
    down_sent = dot(hid_other, d_tok, ((0,), (0,))).astype(BF16)
    up_back = swap(up_sent, "dp", dp, 1)
    down_back = swap(down_sent, "dp", dp, 1)
    g_up = dot(tokens, dpre_own, ((0,), (0,))) + up_back.astype(F32)
    g_down = dot(hid_own, d_tok, ((0,), (0,))) + down_back.astype(F32)
    grad_up = (
        lax.all_to_all(g_up.astype(BF16).reshape(dp, d_rows, f), "dp", 0, 0, tiled=True)
        .transpose(1, 0, 2)
        .reshape(d_rows, ff_m)
        .astype(F32)
    )
    grad_down = (
        lax.all_to_all(
            g_down.astype(BF16).reshape(f, dp, d_rows).transpose(1, 0, 2), "dp", 0, 0, tiled=True
        )
        .reshape(ff_m, d_rows)
        .astype(F32)
    )
    block_out = (joined32 + gate * branch).astype(BF16)
    d_normed = d_mod * (1.0 + scale)
    d_full = d_out32 + inv_std * (
        d_normed
        - jnp.mean(d_normed, axis=-1, keepdims=True)
        - normed * jnp.mean(d_normed * normed, axis=-1, keepdims=True)
    )
    null_part = jnp.where(dropped, d_full[:n_text], F32(0.0)).astype(BF16)
    null_sum = lax.psum(null_part, "dp")

    def whole(rows):
        every = lax.all_gather(rows, "mp", axis=0)
        return jnp.concatenate(
            [every[:, :n_text].reshape(-1, width), every[:, n_text:].reshape(-1, width)], axis=0
        )[None]

    grad_null = lax.all_gather(null_sum, "mp", axis=0, tiled=True).astype(F32)
    return (whole(block_out), whole(d_full.astype(BF16)), grad_up, grad_down, grad_null)


def solution(mesh):
    placed = (
        P("dp", None, None),
        P("dp", None, None),
        P(),
        P("dp"),
        P("dp"),
        P(),
        P("dp", "mp"),
        P("mp", "dp"),
        P("dp", None, None),
    )
    return jax.shard_map(
        functools.partial(shards, mesh.shape["dp"], mesh.shape["mp"]),
        mesh=mesh,
        in_specs=placed,
        out_specs=(P("dp", None, None), P("dp", None, None), P("dp", "mp"), P("mp", "dp"), P()),
        check_vma=False,
    )
```

profile of v0, /device:TPU:0, one launch (start us, length us, event | category | flops | bytes accessed | tf_op | source)
XLA Modules:
  0.0 627.2 jit_solution(12918581351889117631)
XLA Ops:
  13.5 7.3 %all-to-all-start.1 = ((bf16[8,384,384]{2,1,0:T(8,128)(2,1)}), bf16[8,384,384]{2,1,0:T(8,128)(2,1)S(1)}, u32[]{:S(2)}, u32[]{:S(2)}) async-start(bf16[8,384,384]{2,1,0:T(8,128)(2,1)} %bitcast.115), calls=%async_computation.1 | async-start | bytes 4718592 | tf_op jit(solution)/shard_map/all_to_all | solution.py:51
  22.8 68.6 %all-gather.5.cloned.1.call-done = bf16[256,3072]{1,0:T(8,128)(2,1)} async-done(((bf16[64,3072]{1,0:T(8,128)(2,1)}), bf16[256,3072]{1,0:T(8,128)(2,1)}) %all-gather.5.cloned.1.call-update) | async-done | bytes 1572880 | tf_op jit(solution)/shard_map/all_gather | solution.py:79
  92.9 35.0 %all-gather.9.cloned.1.call-done = bf16[256,3072]{1,0:T(8,128)(2,1)} async-done(((bf16[64,3072]{1,0:T(8,128)(2,1)}), bf16[256,3072]{1,0:T(8,128)(2,1)}) %all-gather.9.cloned.1.call-update) | async-done | bytes 1572880 | tf_op jit(solution)/shard_map/all_gather | solution.py:79
  129.3 4.3 copy.23
  135.1 4.4 all-to-all-start
  139.5 3.9 pad_maximum_fusion
  143.4 20.1 %collective-permute-done.6 = bf16[256,3072]{1,0:T(8,128)(2,1)} collective-permute-done((bf16[256,3072]{1,0:T(8,128)(2,1)}, bf16[256,3072]{1,0:T(8,128)(2,1)}, u32[]{:S(2)}, u32[]{:S(2)}) %collective-permute-start.6) | collective-permute-done | bytes 1572896 | tf_op jit(solution)/shard_map/ppermute | solution.py:21
  163.4 3.3 pad_maximum_fusion.1
  168.0 3.0 copy.25
  180.6 11.9 %all-to-all-done = bf16[8,384,384]{1,2,0:T(8,128)(2,1)} async-done(((bf16[8,384,384]{1,2,0:T(8,128)(2,1)}), bf16[8,384,384]{1,2,0:T(8,128)(2,1)}, u32[]{:S(2)}, u32[]{:S(2)}) %all-to-all-start) | async-done | bytes 2359328 | tf_op jit(solution)/shard_map/all_to_all | solution.py:47
  192.5 4.3 copy.24
  198.2 3.8 constant_dynamic-update-slice_fusion
  202.0 3.9 constant_dynamic-update-slice_fusion.3
  205.9 5.6 fusion.46
  211.5 17.3 %collective-permute-done.3 = bf16[384,3072]{0,1:T(8,128)(2,1)} collective-permute-done((bf16[384,3072]{0,1:T(8,128)(2,1)S(1)}, bf16[384,3072]{0,1:T(8,128)(2,1)}, u32[]{:S(2)}, u32[]{:S(2)}) %collective-permute-start.3) | collective-permute-done | bytes 2359328 | tf_op jit(solution)/shard_map/ppermute | solution.py:21
  228.8 6.2 fusion.47
  235.1 4.3 fusion.8
  239.4 39.6 %collective-permute-done.2 = bf16[3072,384]{1,0:T(8,128)(2,1)S(1)} collective-permute-done((bf16[3072,384]{1,0:T(8,128)(2,1)}, bf16[3072,384]{1,0:T(8,128)(2,1)S(1)}, u32[]{:S(2)}, u32[]{:S(2)}) %collective-permute-start.2) | collective-permute-done | bytes 2359328 | tf_op jit(solution)/shard_map/ppermute | solution.py:21
  279.0 4.3 fusion.15
  283.4 4.2 convolution_convert_fusion.1
  291.9 3.5 add_convert_fusion
  297.3 5.2 add_convert_fusion.1
  303.0 4.4 fusion.32
  307.4 4.5 fusion.39
  311.8 29.3 %collective-permute-done.10 = bf16[3072,384]{1,0:T(8,128)(2,1)S(1)} collective-permute-done((bf16[3072,384]{1,0:T(8,128)(2,1)S(1)}, bf16[3072,384]{1,0:T(8,128)(2,1)S(1)}, u32[]{:S(2)}, u32[]{:S(2)}) %collective-permute-start.10) | collective-permute-done | bytes 2359328 | tf_op jit(solution)/shard_map/ppermute | solution.py:21
  341.1 4.8 add_convert_fusion.3
  345.9 6.9 %all-to-all-start.4 = ((bf16[8,384,384]{2,1,0:T(8,128)(2,1)}), bf16[8,384,384]{2,1,0:T(8,128)(2,1)}, u32[]{:S(2)}, u32[]{:S(2)}) async-start(bf16[8,384,384]{2,1,0:T(8,128)(2,1)} %bitcast.116), calls=%async_computation.4 | async-start | bytes 4718592 | tf_op jit(solution)/shard_map/all_to_all | solution.py:125
  352.8 6.3 %fusion.30 = f32[512,3072]{1,0:T(8,128)} fusion(bf16[3072,384]{1,0:T(8,128)(2,1)} %copy-done.2, bf16[1024,384]{1,0:T(8,128)(2,1)S(1)} %copy-done.15), kind=kOutput, calls=%fused_computation.66 | convolution fusion | flops 1207959552 | bytes 9043968 | tf_op jit(solution)/shard_map/dot_general | solution.py:17
  359.2 8.1 %convert_add_fusion = f32[512,3072]{1,0:T(8,128)} fusion(bf16[512,3072]{1,0:T(8,128)(2,1)} %collective-permute-done.8, f32[512,3072]{1,0:T(8,128)S(1)} %bitcast.86, f32[512,3072]{1,0:T(8,128)} %fusion.30), kind=kLoop, calls=%fused_computation | loop fusion | flops 4718592 | bytes 22020096 | tf_op jit(solution)/shard_map/add | solution.py:91
  367.3 3.4 slice.154
  372.2 3.6 fusion.37
  375.9 6.8 %convert_add_fusion.1 = f32[512,3072]{1,0:T(8,128)} fusion(bf16[512,3072]{1,0:T(8,128)(2,1)} %collective-permute-done.4, f32[512,3072]{1,0:T(8,128)S(1)} %bitcast.84, f32[512,3072]{1,0:T(8,128)S(1)} %fusion.37), kind=kLoop, calls=%fused_computation.2 | loop fusion | flops 4718592 | bytes 22020096 | tf_op jit(solution)/shard_map/add | solution.py:91
  382.7 3.2 slice.155
  386.5 21.8 %collective-permute-done.9 = bf16[256,3072]{1,0:T(8,128)(2,1)} collective-permute-done((bf16[256,3072]{1,0:T(8,128)(2,1)}, bf16[256,3072]{1,0:T(8,128)(2,1)}, u32[]{:S(2)}, u32[]{:S(2)}) %collective-permute-start.9) | collective-permute-done | bytes 1572896 | tf_op jit(solution)/shard_map/ppermute | solution.py:21
  408.3 3.9 fusion
  412.3 5.2 all-to-all-start.3
  417.5 7.2 %convolution_convert_fusion = bf16[384,3072]{1,0:T(8,128)(2,1)} fusion(bf16[1024,384]{1,0:T(8,128)(2,1)} %copy-done.13, bf16[1024,3072]{1,0:T(8,128)(2,1)} %constant_dynamic-update-slice_fusion.3), kind=kOutput, calls=%fused_computation.7 | convolution fusion | flops 2417098752 | bytes 9437184 | tf_op jit(solution)/shard_map/dot_general | solution.py:17
  428.1 11.5 %collective-permute-done.5 = bf16[256,3072]{1,0:T(8,128)(2,1)} collective-permute-done((bf16[256,3072]{1,0:T(8,128)(2,1)}, bf16[256,3072]{1,0:T(8,128)(2,1)}, u32[]{:S(2)}, u32[]{:S(2)}) %collective-permute-start.5) | collective-permute-done | bytes 1572896 | tf_op jit(solution)/shard_map/ppermute | solution.py:21
  442.6 6.9 %all-to-all-done.3 = bf16[4,64,3072]{2,1,0:T(8,128)(2,1)} async-done(((bf16[4,64,3072]{2,1,0:T(8,128)(2,1)}), bf16[4,64,3072]{2,1,0:T(8,128)(2,1)}, u32[]{:S(2)}, u32[]{:S(2)}) %all-to-all-start.3) | async-done | bytes 1572896 | tf_op jit(solution)/shard_map/all_to_all | solution.py:95
  449.4 3.6 all-to-all-start.2
  453.3 19.4 %collective-permute-done.11 = bf16[384,3072]{1,0:T(8,128)(2,1)} collective-permute-done((bf16[384,3072]{1,0:T(8,128)(2,1)}, bf16[384,3072]{1,0:T(8,128)(2,1)}, u32[]{:S(2)}, u32[]{:S(2)}) %collective-permute-start.11) | collective-permute-done | bytes 2359328 | tf_op jit(solution)/shard_map/ppermute | solution.py:21
  472.7 6.1 add_convert_fusion.2
  489.3 3.6 all-to-all-start.5
  501.5 46.0 %all-to-all-done.5 = bf16[8,384,384]{2,1,0:T(8,128)(2,1)S(1)} async-done(((bf16[8,384,384]{2,1,0:T(8,128)(2,1)}), bf16[8,384,384]{2,1,0:T(8,128)(2,1)S(1)}, u32[]{:S(2)}, u32[]{:S(2)}) %all-to-all-start.5) | async-done | bytes 2359328 | tf_op jit(solution)/shard_map/all_to_all | solution.py:131
  550.3 25.2 %all-reduce.2.cloned.1.call-done = bf16[16,3072]{1,0:T(8,128)(2,1)} async-done(((bf16[16,3072]{1,0:T(8,128)(2,1)}), bf16[16,3072]{1,0:T(8,128)(2,1)}) %all-reduce.2.cloned.1.call-update) | async-done | bytes 98320 | tf_op jit(solution)/shard_map/psum | solution.py:145
  575.5 6.6 %all_gather.21 = bf16[64,3072]{1,0:T(8,128)(2,1)S(1)} all-gather(bf16[16,3072]{1,0:T(8,128)(2,1)} %all-reduce.2.cloned.1.call-done), channel_id=1, replica_groups=mesh['dp'=8,'mp'=4] {'mp'}, dimensions={0}, use_global_device_ids=true | all-gather | bytes 491520 | tf_op jit(solution)/shard_map/all_gather | solution.py:153
  583.0 13.1 %all-gather.7.cloned.1.call-done = bf16[4,64,3072]{2,1,0:T(8,128)(2,1)} async-done(((bf16[1,64,3072]{2,1,0:T(8,128)(2,1)}), bf16[4,64,3072]{2,1,0:T(8,128)(2,1)}) %all-gather.7.cloned.1.call-update) | async-done | bytes 1572880 | tf_op jit(solution)/shard_map/all_gather | solution.py:148
  598.8 19.0 %all-gather.11.cloned.1.call-done = bf16[4,64,3072]{2,1,0:T(8,128)(2,1)} async-done(((bf16[1,64,3072]{2,1,0:T(8,128)(2,1)}), bf16[4,64,3072]{2,1,0:T(8,128)(2,1)}) %all-gather.11.cloned.1.call-update) | async-done | bytes 1572880 | tf_op jit(solution)/shard_map/all_gather | solution.py:148
  (142 shorter events, 66.8 us)
Async XLA Ops:
  7.2 84.3 %all-gather.5.cloned.1.call-start = ((), (), s32[]{:S(2)}) async-start(), calls=%async_computation.6 | async-start | bytes 1966080 | tf_op jit(solution)/shard_map/all_gather | solution.py:79
  9.6 12.3 %copy-start.8 = (bf16[1,48,3072]{2,1,0:T(8,128)(2,1)}, bf16[1,48,3072]{2,1,0:T(8,128)(2,1)S(1)}, u32[]{:S(2)}) copy-start(bf16[1,48,3072]{2,1,0:T(8,128)(2,1)S(1)} %get-tuple-element.19) | copy-start | bytes 884740
  10.9 2.6 copy-start.20
  12.2 9.7 %copy-start.18 = (f32[1,1,3072]{2,0,1:T(1,128)}, f32[1,1,3072]{2,0,1:T(1,128)S(1)}, u32[]{:S(2)}) copy-start(f32[1,1,3072]{2,0,1:T(1,128)S(1)} %get-tuple-element.12) | copy-start | bytes 36868
  13.5 120.1 %all-to-all-start.1 = ((bf16[8,384,384]{2,1,0:T(8,128)(2,1)}), bf16[8,384,384]{2,1,0:T(8,128)(2,1)S(1)}, u32[]{:S(2)}, u32[]{:S(2)}) async-start(bf16[8,384,384]{2,1,0:T(8,128)(2,1)} %bitcast.115), calls=%async_computation.1 | async-start | bytes 4718592 | tf_op jit(solution)/shard_map/all_to_all | solution.py:51
  20.9 107.0 %all-gather.9.cloned.1.call-start = ((), (), s32[]{:S(2)}) async-start(), calls=%async_computation.8 | async-start | bytes 1966080 | tf_op jit(solution)/shard_map/all_gather | solution.py:79
  21.9 111.7 %copy-start.12 = (bf16[1,64,3072]{2,1,0:T(8,128)(2,1)}, bf16[1,64,3072]{2,1,0:T(8,128)(2,1)S(1)}, u32[]{:S(2)}) copy-start(bf16[1,64,3072]{2,1,0:T(8,128)(2,1)S(1)} %slice.82) | copy-start | bytes 1179652
  91.4 48.0 %collective-permute-start = (bf16[256,3072]{1,0:T(8,128)(2,1)}, bf16[256,3072]{1,0:T(8,128)(2,1)}, u32[]{:S(2)}, u32[]{:S(2)}) collective-permute-start(bf16[256,3072]{1,0:T(8,128)(2,1)} %all-gather.5.cloned.1.call-done), channel_id=1, source_target_pairs={{0,2},{1,3},{2,0},{3,1},{4,6},{5,7},{6,4},{7,5},{8,10},{9,11},{10,... | collective-permute-start | bytes 4718600 | tf_op jit(solution)/shard_map/ppermute | solution.py:21
  127.9 35.6 %collective-permute-start.6 = (bf16[256,3072]{1,0:T(8,128)(2,1)}, bf16[256,3072]{1,0:T(8,128)(2,1)}, u32[]{:S(2)}, u32[]{:S(2)}) collective-permute-start(bf16[256,3072]{1,0:T(8,128)(2,1)} %all-gather.9.cloned.1.call-done), channel_id=1, source_target_pairs={{0,2},{1,3},{2,0},{3,1},{4,6},{5,7},{6,4},{7,5},{8,10},{9,11},{10,... | collective-permute-start | bytes 4718600 | tf_op jit(solution)/shard_map/ppermute | solution.py:21
  135.1 57.4 %all-to-all-start = ((bf16[8,384,384]{1,2,0:T(8,128)(2,1)}), bf16[8,384,384]{1,2,0:T(8,128)(2,1)}, u32[]{:S(2)}, u32[]{:S(2)}) async-start(bf16[8,384,384]{1,2,0:T(8,128)(2,1)} %bitcast.103), calls=%async_computation | async-start | bytes 4718592 | tf_op jit(solution)/shard_map/all_to_all | solution.py:47
  139.5 24.0 %copy-start.7 = (bf16[256,3072]{1,0:T(8,128)(2,1)S(1)}, bf16[256,3072]{1,0:T(8,128)(2,1)}, u32[]{:S(2)}) copy-start(bf16[256,3072]{1,0:T(8,128)(2,1)} %all-gather.9.cloned.1.call-done) | copy-start | bytes 4718596
  143.3 23.4 %copy-start.6 = (bf16[256,3072]{1,0:T(8,128)(2,1)S(1)}, bf16[256,3072]{1,0:T(8,128)(2,1)}, u32[]{:S(2)}) copy-start(bf16[256,3072]{1,0:T(8,128)(2,1)} %all-gather.5.cloned.1.call-done) | copy-start | bytes 4718596
  143.4 54.9 %collective-permute-start.1 = (bf16[512,3072]{1,0:T(8,128)(2,1)}, bf16[512,3072]{1,0:T(8,128)(2,1)}, u32[]{:S(2)}, u32[]{:S(2)}) collective-permute-start(bf16[512,3072]{1,0:T(8,128)(2,1)} %pad_maximum_fusion), channel_id=1, source_target_pairs={{0,1},{1,0},{2,3},{3,2},{4,5},{5,4},{6,7},{7,6},{8,9},{9,8},{10,11... | collective-permute-start | bytes 9437192 | tf_op jit(solution)/shard_map/ppermute | solution.py:21
  166.7 35.3 %collective-permute-start.7 = (bf16[512,3072]{1,0:T(8,128)(2,1)}, bf16[512,3072]{1,0:T(8,128)(2,1)}, u32[]{:S(2)}, u32[]{:S(2)}) collective-permute-start(bf16[512,3072]{1,0:T(8,128)(2,1)} %pad_maximum_fusion.1), channel_id=1, source_target_pairs={{0,1},{1,0},{2,3},{3,2},{4,5},{5,4},{6,7},{7,6},{8,9},{9,8},{10,11... | collective-permute-start | bytes 9437192 | tf_op jit(solution)/shard_map/ppermute | solution.py:21
  171.0 57.8 %collective-permute-start.3 = (bf16[384,3072]{0,1:T(8,128)(2,1)S(1)}, bf16[384,3072]{0,1:T(8,128)(2,1)}, u32[]{:S(2)}, u32[]{:S(2)}) collective-permute-start(bf16[384,3072]{0,1:T(8,128)(2,1)S(1)} %bitcast.87), channel_id=1, source_target_pairs={{0,4},{4,0},{8,12},{12,8},{16,20},{20,16},{24,28},{28,24},{1,5},{5... | collective-permute-start | bytes 7077896 | tf_op jit(solution)/shard_map/ppermute | solution.py:21
  196.8 82.3 %collective-permute-start.2 = (bf16[3072,384]{1,0:T(8,128)(2,1)}, bf16[3072,384]{1,0:T(8,128)(2,1)S(1)}, u32[]{:S(2)}, u32[]{:S(2)}) collective-permute-start(bf16[3072,384]{1,0:T(8,128)(2,1)} %bitcast.91), channel_id=1, source_target_pairs={{0,4},{4,0},{8,12},{12,8},{16,20},{20,16},{24,28},{28,24},{1,5},{5... | collective-permute-start | bytes 7077896 | tf_op jit(solution)/shard_map/ppermute | solution.py:21
  205.9 29.2 %slice-start.11 = ((s8[6291456]{0:T(1024)(128)(4,1)}), s8[4194304]{0:T(1024)(128)(4,1)S(1)}, s32[]{:S(2)}) async-start(s8[6291456]{0:T(1024)(128)(4,1)} %bitcast.117), calls=%async_computation.22 | async-start | bytes 8388608
  211.5 23.6 %copy-start = (bf16[8,384,384]{2,1,0:T(8,128)(2,1)S(1)}, bf16[8,384,384]{2,1,0:T(8,128)(2,1)}, u32[]{:S(2)}) copy-start(bf16[8,384,384]{2,1,0:T(8,128)(2,1)} %copy.24) | copy-start | bytes 7077892
  211.5 23.6 %slice-start.12 = ((s8[6291456]{0:T(1024)(128)(4,1)}), s8[2097152]{0:T(1024)(128)(4,1)S(1)}, s32[]{:S(2)}) async-start(s8[6291456]{0:T(1024)(128)(4,1)} %bitcast.117), calls=%async_computation.23 | async-start | bytes 4194304
  239.4 67.9 %copy-start.10 = (bf16[1024,384]{1,0:T(8,128)(2,1)}, bf16[1024,384]{1,0:T(8,128)(2,1)S(1)}, u32[]{:S(2)}) copy-start(bf16[1024,384]{1,0:T(8,128)(2,1)S(1)} %get-tuple-element.11) | copy-start | bytes 2359300
  279.0 12.9 %copy-start.2 = (bf16[3072,384]{1,0:T(8,128)(2,1)}, bf16[3072,384]{1,0:T(8,128)(2,1)S(1)}, u32[]{:S(2)}) copy-start(bf16[3072,384]{1,0:T(8,128)(2,1)S(1)} %collective-permute-done.2) | copy-start | bytes 7077892
  283.4 8.5 %copy-start.14 = (bf16[1024,384]{1,0:T(8,128)(2,1)}, bf16[1024,384]{1,0:T(8,128)(2,1)S(1)}, u32[]{:S(2)}) copy-start(bf16[1024,384]{1,0:T(8,128)(2,1)S(1)} %get-tuple-element.8) | copy-start | bytes 2359300
  283.4 13.9 %copy-start.13 = (bf16[1024,384]{1,0:T(8,128)(2,1)}, bf16[1024,384]{1,0:T(8,128)(2,1)S(1)}, u32[]{:S(2)}) copy-start(bf16[1024,384]{1,0:T(8,128)(2,1)S(1)} %get-tuple-element.9) | copy-start | bytes 2359300
  287.6 53.5 %collective-permute-start.10 = (bf16[3072,384]{1,0:T(8,128)(2,1)S(1)}, bf16[3072,384]{1,0:T(8,128)(2,1)S(1)}, u32[]{:S(2)}, u32[]{:S(2)}) collective-permute-start(bf16[3072,384]{1,0:T(8,128)(2,1)S(1)} %convolution_convert_fusion.1), channel_id=1, source_target_pairs={{0,4},{4,0},{8,12},{12,8},{16,20},{20,16},{24,28},{28,24},{1,5},{5... | collective-permute-start | bytes 7077896 | tf_op jit(solution)/shard_map/ppermute | solution.py:21
  295.4 63.8 %collective-permute-start.8 = (bf16[512,3072]{1,0:T(8,128)(2,1)}, bf16[512,3072]{1,0:T(8,128)(2,1)}, u32[]{:S(2)}, u32[]{:S(2)}) collective-permute-start(bf16[512,3072]{1,0:T(8,128)(2,1)} %add_convert_fusion), channel_id=1, source_target_pairs={{0,1},{1,0},{2,3},{3,2},{4,5},{5,4},{6,7},{7,6},{8,9},{9,8},{10,11... | collective-permute-start | bytes 9437192 | tf_op jit(solution)/shard_map/ppermute | solution.py:21
  302.5 73.4 %collective-permute-start.4 = (bf16[512,3072]{1,0:T(8,128)(2,1)}, bf16[512,3072]{1,0:T(8,128)(2,1)}, u32[]{:S(2)}, u32[]{:S(2)}) collective-permute-start(bf16[512,3072]{1,0:T(8,128)(2,1)} %add_convert_fusion.1), channel_id=1, source_target_pairs={{0,1},{1,0},{2,3},{3,2},{4,5},{5,4},{6,7},{7,6},{8,9},{9,8},{10,11... | collective-permute-start | bytes 9437192 | tf_op jit(solution)/shard_map/ppermute | solution.py:21
  345.9 6.9 %copy-start.15 = (bf16[1024,384]{1,0:T(8,128)(2,1)S(1)}, bf16[1024,384]{1,0:T(8,128)(2,1)}, u32[]{:S(2)}) copy-start(bf16[1024,384]{1,0:T(8,128)(2,1)} %copy-done.14) | copy-start | bytes 2359300
  345.9 13.3 %slice-start.2 = ((s8[6291456]{0:T(1024)(128)(4,1)}), s8[2097152]{0:T(1024)(128)(4,1)S(1)}, s32[]{:S(2)}) async-start(s8[6291456]{0:T(1024)(128)(4,1)} %bitcast.85), calls=%async_computation.13 | async-start | bytes 4194304
  345.9 66.3 %all-to-all-start.4 = ((bf16[8,384,384]{2,1,0:T(8,128)(2,1)}), bf16[8,384,384]{2,1,0:T(8,128)(2,1)}, u32[]{:S(2)}, u32[]{:S(2)}) async-start(bf16[8,384,384]{2,1,0:T(8,128)(2,1)} %bitcast.116), calls=%async_computation.4 | async-start | bytes 4718592 | tf_op jit(solution)/shard_map/all_to_all | solution.py:125
  352.8 6.4 %slice-start.3 = ((s8[6291456]{0:T(1024)(128)(4,1)}), s8[4194304]{0:T(1024)(128)(4,1)S(1)}, s32[]{:S(2)}) async-start(s8[6291456]{0:T(1024)(128)(4,1)} %bitcast.85), calls=%async_computation.14 | async-start | bytes 8388608
  367.3 8.5 %slice-start = ((s8[6291456]{0:T(1024)(128)(4,1)}), s8[4194304]{0:T(1024)(128)(4,1)S(1)}, s32[]{:S(2)}) async-start(s8[6291456]{0:T(1024)(128)(4,1)} %bitcast.83), calls=%async_computation.11 | async-start | bytes 8388608
  370.7 5.1 slice-start.1
  370.7 37.6 %collective-permute-start.9 = (bf16[256,3072]{1,0:T(8,128)(2,1)}, bf16[256,3072]{1,0:T(8,128)(2,1)}, u32[]{:S(2)}, u32[]{:S(2)}) collective-permute-start(bf16[256,3072]{1,0:T(8,128)(2,1)} %slice.154), channel_id=1, source_target_pairs={{0,2},{1,3},{2,0},{3,1},{4,6},{5,7},{6,4},{7,5},{8,10},{9,11},{10,... | collective-permute-start | bytes 4718600 | tf_op jit(solution)/shard_map/ppermute | solution.py:21
  385.9 53.6 %collective-permute-start.5 = (bf16[256,3072]{1,0:T(8,128)(2,1)}, bf16[256,3072]{1,0:T(8,128)(2,1)}, u32[]{:S(2)}, u32[]{:S(2)}) collective-permute-start(bf16[256,3072]{1,0:T(8,128)(2,1)} %slice.155), channel_id=1, source_target_pairs={{0,2},{1,3},{2,0},{3,1},{4,6},{5,7},{6,4},{7,5},{8,10},{9,11},{10,... | collective-permute-start | bytes 4718600 | tf_op jit(solution)/shard_map/ppermute | solution.py:21
  412.3 27.3 %slice-start.4 = ((s8[6291456]{0:T(1024)(128)(4,1)}), s8[2097152]{0:T(1024)(128)(4,1)S(1)}, s32[]{:S(2)}) async-start(s8[6291456]{0:T(1024)(128)(4,1)} %bitcast.95), calls=%async_computation.15 | async-start | bytes 4194304
  412.3 37.2 %all-to-all-start.3 = ((bf16[4,64,3072]{2,1,0:T(8,128)(2,1)}), bf16[4,64,3072]{2,1,0:T(8,128)(2,1)}, u32[]{:S(2)}, u32[]{:S(2)}) async-start(bf16[4,64,3072]{2,1,0:T(8,128)(2,1)} %bitcast.106), calls=%async_computation.3 | async-start | bytes 3145728 | tf_op jit(solution)/shard_map/all_to_all | solution.py:95
  417.5 9.6 %copy-start.9 = (bf16[1,48,3072]{2,1,0:T(8,128)(2,1)S(1)}, bf16[1,48,3072]{2,1,0:T(8,128)(2,1)}, u32[]{:S(2)}) copy-start(bf16[1,48,3072]{2,1,0:T(8,128)(2,1)} %copy-done.8) | copy-start | bytes 884740
  417.5 22.1 %slice-start.5 = ((s8[6291456]{0:T(1024)(128)(4,1)}), s8[4194304]{0:T(1024)(128)(4,1)S(1)}, s32[]{:S(2)}) async-start(s8[6291456]{0:T(1024)(128)(4,1)} %bitcast.95), calls=%async_computation.16 | async-start | bytes 8388608
  424.7 48.0 %collective-permute-start.11 = (bf16[384,3072]{1,0:T(8,128)(2,1)}, bf16[384,3072]{1,0:T(8,128)(2,1)}, u32[]{:S(2)}, u32[]{:S(2)}) collective-permute-start(bf16[384,3072]{1,0:T(8,128)(2,1)} %convolution_convert_fusion), channel_id=1, source_target_pairs={{0,4},{4,0},{8,12},{12,8},{16,20},{20,16},{24,28},{28,24},{1,5},{5... | collective-permute-start | bytes 7077896 | tf_op jit(solution)/shard_map/ppermute | solution.py:21
  442.6 30.1 %copy-start.11 = (bf16[1024,384]{1,0:T(8,128)(2,1)S(1)}, bf16[1024,384]{1,0:T(8,128)(2,1)}, u32[]{:S(2)}) copy-start(bf16[1024,384]{1,0:T(8,128)(2,1)} %copy-done.10) | copy-start | bytes 2359300
  449.4 38.7 %all-to-all-start.2 = ((bf16[4,64,3072]{2,1,0:T(8,128)(2,1)}), bf16[4,64,3072]{2,1,0:T(8,128)(2,1)S(1)}, u32[]{:S(2)}, u32[]{:S(2)}) async-start(bf16[4,64,3072]{2,1,0:T(8,128)(2,1)} %bitcast.105), calls=%async_computation.2 | async-start | bytes 3145728 | tf_op jit(solution)/shard_map/all_to_all | solution.py:95
  453.0 122.5 %all-reduce.2.cloned.1.call-start = ((), (), s32[]{:S(2)}) async-start(), calls=%async_computation.10 | async-start | bytes 196608 | tf_op jit(solution)/shard_map/psum | solution.py:145
  478.8 4.3 copy-start.17
  478.8 4.3 copy-start.21
  478.9 4.3 copy-start.23
  489.3 58.2 %all-to-all-start.5 = ((bf16[8,384,384]{2,1,0:T(8,128)(2,1)}), bf16[8,384,384]{2,1,0:T(8,128)(2,1)S(1)}, u32[]{:S(2)}, u32[]{:S(2)}) async-start(bf16[8,384,384]{2,1,0:T(8,128)(2,1)} %bitcast.101), calls=%async_computation.5 | async-start | bytes 4718592 | tf_op jit(solution)/shard_map/all_to_all | solution.py:131
  492.9 103.2 %all-gather.7.cloned.1.call-start = ((), (), s32[]{:S(2)}) async-start(), calls=%async_computation.7 | async-start | bytes 1966080 | tf_op jit(solution)/shard_map/all_gather | solution.py:148
  496.1 121.7 %all-gather.11.cloned.1.call-start = ((), (), s32[]{:S(2)}) async-start(), calls=%async_computation.9 | async-start | bytes 1966080 | tf_op jit(solution)/shard_map/all_gather | solution.py:148
  (12 other events, 17.1 us)
Sparse Core Ops, SparseCore 0:
  13.6 77.7 all-gather.4
  93.6 34.2 all-gather.8
  485.4 90.0 all-reduce.1
  577.5 18.6 all-gather.6
  598.1 19.6 all-gather.10
where the time goes:
time: 638 us; the launch traced here: 627 us
  waiting for transfers between devices  388 us (61%)
  matrix products  74.1 us (12%)
  other arithmetic  49.7 us (8%)
  local copies, waits for them, and re-layouts  49 us (8%)
  starting transfers between devices  43.8 us (7%)
  between operations  15.9 us (2%)
  blocking collectives  6.63 us (1%)
    ppermute x12, waiting for transfers between devices, swap(): return lax.ppermute(values, axis, [(i, i ^ bit) for i in range(size)])  159 us
    all_gather x2, waiting for transfers between devices, gather(): lax.all_gather(rows, 'dp', axis=0, tiled=True, axis_index_groups=lines)  104 us
    dot_general x16, matrix products, dot(): lax.dot_general(left, right, (dims, ((), ())), preferred_element_type=F32)  74.1 us
    all_to_all x1, waiting for transfers between devices, shards(): lax.all_to_all(g_down.astype(BF16).reshape(f, dp, d_rows).transpose(1, 0,...  46 us
    all_gather x2, waiting for transfers between devices, whole(): every = lax.all_gather(rows, 'mp', axis=0)  32.1 us
    psum x1, waiting for transfers between devices, shards(): null_sum = lax.psum(null_part, 'dp')  25.2 us
    unnamed x69, local copies, waits for them, and re-layouts  17.3 us
    add x2, other arithmetic, scatter(): total = product(slice(0, half)) + sent.astype(F32)  14.9 us
  transfers between devices with their start and end apart: 23, of which 16 were waited for; matrix products, arithmetic and copies ran while one was open for 24% of the time, Pallas kernels for 0%

commit v1 on v0

--- a/solution.py
+++ b/solution.py
@@ -7,6 +7,12 @@
 EPS = 1e-06
 BF16 = jnp.bfloat16
 F32 = jnp.float32
+
+
+def summed_here(x, mesh_axis):
+    pieces = lax.all_gather(x, mesh_axis, axis=0, tiled=False)
+    result = pieces.sum(axis=0)
+    return result
 
 
 def gelu_tanh(values):
@@ -142,7 +148,7 @@
         - normed * jnp.mean(d_normed * normed, axis=-1, keepdims=True)
     )
     null_part = jnp.where(dropped, d_full[:n_text], F32(0.0)).astype(BF16)
-    null_sum = lax.psum(null_part, "dp")
+    null_sum = summed_here(null_part, "dp")
 
     def whole(rows):
         every = lax.all_gather(rows, "mp", axis=0)

time: 638 us -> 612 us (0.959)
  waiting for transfers between devices: 388 us -> 334 us
  blocking collectives: 6.63 us -> 38.5 us
    all_gather x2, waiting for transfers between devices: 32.1 us -> 0.01 us  [whole(): every = lax.all_gather(rows, 'mp', axis=0)]
    all_gather x0 -> x1, blocking collectives: none -> 32.1 us  [summed_here(): pieces = lax.all_gather(x, mesh_axis, axis=0, tiled=False)]
    psum x1 -> x0, waiting for transfers between devices: 25.2 us -> none  [shards(): null_sum = lax.psum(null_part, 'dp')]
    unnamed x69 -> x79, local copies, waits for them, and re-layouts: 17.3 us -> 16.4 us
  transfers between devices with their start and end apart: 23 -> 22, of which waited for: 16 -> 13; matrix products, arithmetic and copies ran while one was open for 24% -> 25% of each run, Pallas kernels for 0% -> 0%
where the time goes in v1:
time: 612 us; the launch traced here: 602 us
  waiting for transfers between devices  334 us (55%)
  matrix products  73.9 us (12%)
  local copies, waits for them, and re-layouts  48.3 us (8%)
  other arithmetic  47.7 us (8%)
  starting transfers between devices  43.9 us (7%)
  blocking collectives  38.5 us (6%)
  between operations  16 us (3%)
    ppermute x12, waiting for transfers between devices, swap(): return lax.ppermute(values, axis, [(i, i ^ bit) for i in range(size)])  160 us
    all_gather x2, waiting for transfers between devices, gather(): lax.all_gather(rows, 'dp', axis=0, tiled=True, axis_index_groups=lines)  104 us
    dot_general x16, matrix products, dot(): lax.dot_general(left, right, (dims, ((), ())), preferred_element_type=F32)  73.9 us
    all_to_all x1, waiting for transfers between devices, shards(): lax.all_to_all(g_down.astype(BF16).reshape(f, dp, d_rows).transpose(1, 0,...  43.5 us
    all_gather x1, blocking collectives, summed_here(): pieces = lax.all_gather(x, mesh_axis, axis=0, tiled=False)  32.1 us
    unnamed x79, local copies, waits for them, and re-layouts  16.4 us
    all_to_all x2, waiting for transfers between devices, scatter(): lax.all_to_all(total.astype(BF16).reshape(per_line, -1, width), 'dp', 0,...  15 us
    add x2, other arithmetic, scatter(): total = product(slice(0, half)) + sent.astype(F32)  14.9 us
  transfers between devices with their start and end apart: 22, of which 13 were waited for; matrix products, arithmetic and copies ran while one was open for 25% of the time, Pallas kernels for 0%

profile of v1, /device:TPU:0, one launch (start us, length us, event | category | flops | bytes accessed | tf_op | source)
XLA Modules:
  0.0 602.0 jit_solution(2968229161004220025)
XLA Ops:
  13.5 7.3 %all-to-all-start.1 = ((bf16[8,384,384]{2,1,0:T(8,128)(2,1)}), bf16[8,384,384]{2,1,0:T(8,128)(2,1)S(1)}, u32[]{:S(2)}, u32[]{:S(2)}) async-start(bf16[8,384,384]{2,1,0:T(8,128)(2,1)} %bitcast.117), calls=%async_computation.1 | async-start | bytes 4718592 | tf_op jit(solution)/shard_map/all_to_all | solution.py:57
  22.8 68.6 %all-gather.6.cloned.1.call-done = bf16[256,3072]{1,0:T(8,128)(2,1)} async-done(((bf16[64,3072]{1,0:T(8,128)(2,1)}), bf16[256,3072]{1,0:T(8,128)(2,1)}) %all-gather.6.cloned.1.call-update) | async-done | bytes 1572880 | tf_op jit(solution)/shard_map/all_gather | solution.py:85
  92.9 35.0 %all-gather.10.cloned.1.call-done = bf16[256,3072]{1,0:T(8,128)(2,1)} async-done(((bf16[64,3072]{1,0:T(8,128)(2,1)}), bf16[256,3072]{1,0:T(8,128)(2,1)}) %all-gather.10.cloned.1.call-update) | async-done | bytes 1572880 | tf_op jit(solution)/shard_map/all_gather | solution.py:85
  129.3 4.3 copy.23
  135.1 4.4 all-to-all-start
  139.5 3.9 pad_maximum_fusion
  143.3 20.1 %collective-permute-done.6 = bf16[256,3072]{1,0:T(8,128)(2,1)} collective-permute-done((bf16[256,3072]{1,0:T(8,128)(2,1)}, bf16[256,3072]{1,0:T(8,128)(2,1)}, u32[]{:S(2)}, u32[]{:S(2)}) %collective-permute-start.6) | collective-permute-done | bytes 1572896 | tf_op jit(solution)/shard_map/ppermute | solution.py:27
  163.4 3.3 pad_maximum_fusion.1
  168.0 3.0 copy.25
  180.6 11.9 %all-to-all-done = bf16[8,384,384]{1,2,0:T(8,128)(2,1)} async-done(((bf16[8,384,384]{1,2,0:T(8,128)(2,1)}), bf16[8,384,384]{1,2,0:T(8,128)(2,1)}, u32[]{:S(2)}, u32[]{:S(2)}) %all-to-all-start) | async-done | bytes 2359328 | tf_op jit(solution)/shard_map/all_to_all | solution.py:53
  192.5 4.3 copy.24
  198.2 3.8 constant_dynamic-update-slice_fusion
  202.0 4.0 constant_dynamic-update-slice_fusion.3
  206.0 5.6 fusion.46
  211.7 17.2 %collective-permute-done.3 = bf16[384,3072]{0,1:T(8,128)(2,1)} collective-permute-done((bf16[384,3072]{0,1:T(8,128)(2,1)S(1)}, bf16[384,3072]{0,1:T(8,128)(2,1)}, u32[]{:S(2)}, u32[]{:S(2)}) %collective-permute-start.3) | collective-permute-done | bytes 2359328 | tf_op jit(solution)/shard_map/ppermute | solution.py:27
  228.8 6.2 %fusion.47 = f32[1024,384]{1,0:T(8,128)S(1)} fusion(bf16[1024,3072]{1,0:T(8,128)(2,1)} %constant_dynamic-update-slice_fusion.3, bf16[384,3072]{0,1:T(8,128)(2,1)} %collective-permute-done.3), kind=kOutput, calls=%fused_computation.107 | convolution fusion | flops 2415919104 | bytes 10223616 | tf_op jit(solution)/shard_map/dot_general | solution.py:23
  235.1 4.3 fusion.8
  239.4 39.6 %collective-permute-done.2 = bf16[3072,384]{1,0:T(8,128)(2,1)S(1)} collective-permute-done((bf16[3072,384]{1,0:T(8,128)(2,1)}, bf16[3072,384]{1,0:T(8,128)(2,1)S(1)}, u32[]{:S(2)}, u32[]{:S(2)}) %collective-permute-start.2) | collective-permute-done | bytes 2359328 | tf_op jit(solution)/shard_map/ppermute | solution.py:27
  279.0 4.3 fusion.15
  283.4 4.2 convolution_convert_fusion.1
  291.9 3.5 add_convert_fusion
  297.3 5.2 add_convert_fusion.1
  303.0 4.4 fusion.32
  307.4 4.5 fusion.39
  311.8 29.3 %collective-permute-done.10 = bf16[3072,384]{1,0:T(8,128)(2,1)S(1)} collective-permute-done((bf16[3072,384]{1,0:T(8,128)(2,1)S(1)}, bf16[3072,384]{1,0:T(8,128)(2,1)S(1)}, u32[]{:S(2)}, u32[]{:S(2)}) %collective-permute-start.10) | collective-permute-done | bytes 2359328 | tf_op jit(solution)/shard_map/ppermute | solution.py:27
  341.1 4.8 add_convert_fusion.3
  345.9 6.9 %all-to-all-start.4 = ((bf16[8,384,384]{2,1,0:T(8,128)(2,1)}), bf16[8,384,384]{2,1,0:T(8,128)(2,1)}, u32[]{:S(2)}, u32[]{:S(2)}) async-start(bf16[8,384,384]{2,1,0:T(8,128)(2,1)} %bitcast.118), calls=%async_computation.4 | async-start | bytes 4718592 | tf_op jit(solution)/shard_map/all_to_all | solution.py:131
  352.8 6.4 %fusion.30 = f32[512,3072]{1,0:T(8,128)} fusion(bf16[3072,384]{1,0:T(8,128)(2,1)} %copy-done.2, bf16[1024,384]{1,0:T(8,128)(2,1)S(1)} %copy-done.15), kind=kOutput, calls=%fused_computation.66 | convolution fusion | flops 1207959552 | bytes 9043968 | tf_op jit(solution)/shard_map/dot_general | solution.py:23
  359.2 8.1 %convert_add_fusion = f32[512,3072]{1,0:T(8,128)} fusion(bf16[512,3072]{1,0:T(8,128)(2,1)} %collective-permute-done.8, f32[512,3072]{1,0:T(8,128)S(1)} %bitcast.87, f32[512,3072]{1,0:T(8,128)} %fusion.30), kind=kLoop, calls=%fused_computation | loop fusion | flops 4718592 | bytes 22020096 | tf_op jit(solution)/shard_map/add | solution.py:97
  367.3 3.4 slice.154
  372.2 3.6 fusion.37
  375.9 6.8 %convert_add_fusion.1 = f32[512,3072]{1,0:T(8,128)} fusion(bf16[512,3072]{1,0:T(8,128)(2,1)} %collective-permute-done.4, f32[512,3072]{1,0:T(8,128)S(1)} %bitcast.85, f32[512,3072]{1,0:T(8,128)S(1)} %fusion.37), kind=kLoop, calls=%fused_computation.2 | loop fusion | flops 4718592 | bytes 22020096 | tf_op jit(solution)/shard_map/add | solution.py:97
  382.7 3.2 slice.155
  386.5 21.8 %collective-permute-done.9 = bf16[256,3072]{1,0:T(8,128)(2,1)} collective-permute-done((bf16[256,3072]{1,0:T(8,128)(2,1)}, bf16[256,3072]{1,0:T(8,128)(2,1)}, u32[]{:S(2)}, u32[]{:S(2)}) %collective-permute-start.9) | collective-permute-done | bytes 1572896 | tf_op jit(solution)/shard_map/ppermute | solution.py:27
  408.3 3.9 fusion
  412.3 5.4 all-to-all-start.3
  417.6 7.0 %convolution_convert_fusion = bf16[384,3072]{1,0:T(8,128)(2,1)} fusion(bf16[1024,384]{1,0:T(8,128)(2,1)S(1)} %copy-done.13, bf16[1024,3072]{1,0:T(8,128)(2,1)} %constant_dynamic-update-slice_fusion.3), kind=kOutput, calls=%fused_computation.7 | convolution fusion | flops 2417098752 | bytes 9437184 | tf_op jit(solution)/shard_map/dot_general | solution.py:23
  426.1 13.5 %collective-permute-done.5 = bf16[256,3072]{1,0:T(8,128)(2,1)} collective-permute-done((bf16[256,3072]{1,0:T(8,128)(2,1)}, bf16[256,3072]{1,0:T(8,128)(2,1)}, u32[]{:S(2)}, u32[]{:S(2)}) %collective-permute-start.5) | collective-permute-done | bytes 1572896 | tf_op jit(solution)/shard_map/ppermute | solution.py:27
  439.6 3.0 fusion.1
  442.6 7.0 %all-to-all-done.3 = bf16[4,64,3072]{2,1,0:T(8,128)(2,1)} async-done(((bf16[4,64,3072]{2,1,0:T(8,128)(2,1)}), bf16[4,64,3072]{2,1,0:T(8,128)(2,1)}, u32[]{:S(2)}, u32[]{:S(2)}) %all-to-all-start.3) | async-done | bytes 1572896 | tf_op jit(solution)/shard_map/all_to_all | solution.py:101
  449.6 3.8 all-to-all-start.2
  454.2 18.3 %collective-permute-done.11 = bf16[384,3072]{1,0:T(8,128)(2,1)} collective-permute-done((bf16[384,3072]{1,0:T(8,128)(2,1)}, bf16[384,3072]{1,0:T(8,128)(2,1)}, u32[]{:S(2)}, u32[]{:S(2)}) %collective-permute-start.11) | collective-permute-done | bytes 2359328 | tf_op jit(solution)/shard_map/ppermute | solution.py:27
  472.6 6.1 %add_convert_fusion.2 = bf16[384,3072]{1,0:T(8,128)(2,1)S(1)} fusion(bf16[384,3072]{1,0:T(8,128)(2,1)} %collective-permute-done.11, bf16[1024,384]{1,0:T(8,128)(2,1)S(1)} %copy-done.10, bf16[1024,3072]{1,0:T(8,128)(2,1)} %constant_dynamic-update-slice_fusion.3), kind=kOutput, calls=%fused_computation.5 | convolution fusion | flops 2419458048 | bytes 11796480 | tf_op jit(solution)/shard_map/dot_general | solution.py:23
  480.4 8.1 %all-to-all-done.2 = bf16[4,64,3072]{2,1,0:T(8,128)(2,1)S(1)} async-done(((bf16[4,64,3072]{2,1,0:T(8,128)(2,1)}), bf16[4,64,3072]{2,1,0:T(8,128)(2,1)S(1)}, u32[]{:S(2)}, u32[]{:S(2)}) %all-to-all-start.2) | async-done | bytes 1572896 | tf_op jit(solution)/shard_map/all_to_all | solution.py:101
  489.6 3.6 all-to-all-start.5
  503.1 43.5 %all-to-all-done.5 = bf16[8,384,384]{2,1,0:T(8,128)(2,1)S(1)} async-done(((bf16[8,384,384]{2,1,0:T(8,128)(2,1)}), bf16[8,384,384]{2,1,0:T(8,128)(2,1)S(1)}, u32[]{:S(2)}, u32[]{:S(2)}) %all-to-all-start.5) | async-done | bytes 2359328 | tf_op jit(solution)/shard_map/all_to_all | solution.py:137
  550.4 32.1 %all-gather = bf16[128,3072]{1,0:T(8,128)(2,1)S(1)} all-gather(bf16[16,3072]{1,0:T(8,128)(2,1)S(1)} %fusion.42), channel_id=2, replica_groups=mesh['dp'=8,'mp'=4] {'dp'}, dimensions={0}, use_global_device_ids=true | all-gather | bytes 884736 | tf_op jit(solution)/shard_map/all_gather | solution.py:13
  582.6 6.4 %all_gather.29 = bf16[64,3072]{1,0:T(8,128)(2,1)S(1)} all-gather(bf16[16,3072]{1,0:T(8,128)(2,1)S(1)} %reduce_sum.78), channel_id=1, replica_groups=mesh['dp'=8,'mp'=4] {'mp'}, dimensions={0}, use_global_device_ids=true | all-gather | bytes 491520 | tf_op jit(solution)/shard_map/all_gather | solution.py:159
  (151 shorter events, 57.4 us)
Async XLA Ops:
  7.2 84.3 %all-gather.6.cloned.1.call-start = ((), (), s32[]{:S(2)}) async-start(), calls=%async_computation.6 | async-start | bytes 1966080 | tf_op jit(solution)/shard_map/all_gather | solution.py:85
  9.6 12.3 %copy-start.7 = (bf16[1,48,3072]{2,1,0:T(8,128)(2,1)}, bf16[1,48,3072]{2,1,0:T(8,128)(2,1)S(1)}, u32[]{:S(2)}) copy-start(bf16[1,48,3072]{2,1,0:T(8,128)(2,1)S(1)} %get-tuple-element.19) | copy-start | bytes 884740
  10.9 2.6 copy-start.20
  11.2 2.3 copy-start.22
  12.2 9.7 %copy-start.18 = (f32[1,1,3072]{2,0,1:T(1,128)}, f32[1,1,3072]{2,0,1:T(1,128)S(1)}, u32[]{:S(2)}) copy-start(f32[1,1,3072]{2,0,1:T(1,128)S(1)} %get-tuple-element.12) | copy-start | bytes 36868
  13.5 120.1 %all-to-all-start.1 = ((bf16[8,384,384]{2,1,0:T(8,128)(2,1)}), bf16[8,384,384]{2,1,0:T(8,128)(2,1)S(1)}, u32[]{:S(2)}, u32[]{:S(2)}) async-start(bf16[8,384,384]{2,1,0:T(8,128)(2,1)} %bitcast.117), calls=%async_computation.1 | async-start | bytes 4718592 | tf_op jit(solution)/shard_map/all_to_all | solution.py:57
  20.9 107.0 %all-gather.10.cloned.1.call-start = ((), (), s32[]{:S(2)}) async-start(), calls=%async_computation.8 | async-start | bytes 1966080 | tf_op jit(solution)/shard_map/all_gather | solution.py:85
  21.9 111.7 %copy-start.11 = (bf16[1,64,3072]{2,1,0:T(8,128)(2,1)}, bf16[1,64,3072]{2,1,0:T(8,128)(2,1)S(1)}, u32[]{:S(2)}) copy-start(bf16[1,64,3072]{2,1,0:T(8,128)(2,1)S(1)} %slice.82) | copy-start | bytes 1179652
  91.4 48.0 %collective-permute-start = (bf16[256,3072]{1,0:T(8,128)(2,1)}, bf16[256,3072]{1,0:T(8,128)(2,1)}, u32[]{:S(2)}, u32[]{:S(2)}) collective-permute-start(bf16[256,3072]{1,0:T(8,128)(2,1)} %all-gather.6.cloned.1.call-done), channel_id=1, source_target_pairs={{0,2},{1,3},{2,0},{3,1},{4,6},{5,7},{6,4},{7,5},{8,10},{9,11},{10,... | collective-permute-start | bytes 4718600 | tf_op jit(solution)/shard_map/ppermute | solution.py:27
  127.9 35.6 %collective-permute-start.6 = (bf16[256,3072]{1,0:T(8,128)(2,1)}, bf16[256,3072]{1,0:T(8,128)(2,1)}, u32[]{:S(2)}, u32[]{:S(2)}) collective-permute-start(bf16[256,3072]{1,0:T(8,128)(2,1)} %all-gather.10.cloned.1.call-done), channel_id=1, source_target_pairs={{0,2},{1,3},{2,0},{3,1},{4,6},{5,7},{6,4},{7,5},{8,10},{9,11},{10,... | collective-permute-start | bytes 4718600 | tf_op jit(solution)/shard_map/ppermute | solution.py:27
  135.1 57.4 %all-to-all-start = ((bf16[8,384,384]{1,2,0:T(8,128)(2,1)}), bf16[8,384,384]{1,2,0:T(8,128)(2,1)}, u32[]{:S(2)}, u32[]{:S(2)}) async-start(bf16[8,384,384]{1,2,0:T(8,128)(2,1)} %bitcast.104), calls=%async_computation | async-start | bytes 4718592 | tf_op jit(solution)/shard_map/all_to_all | solution.py:53
  139.5 24.0 %copy-start.6 = (bf16[256,3072]{1,0:T(8,128)(2,1)S(1)}, bf16[256,3072]{1,0:T(8,128)(2,1)}, u32[]{:S(2)}) copy-start(bf16[256,3072]{1,0:T(8,128)(2,1)} %all-gather.10.cloned.1.call-done) | copy-start | bytes 4718596
  143.3 23.4 %copy-start.5 = (bf16[256,3072]{1,0:T(8,128)(2,1)S(1)}, bf16[256,3072]{1,0:T(8,128)(2,1)}, u32[]{:S(2)}) copy-start(bf16[256,3072]{1,0:T(8,128)(2,1)} %all-gather.6.cloned.1.call-done) | copy-start | bytes 4718596
  143.3 54.9 %collective-permute-start.1 = (bf16[512,3072]{1,0:T(8,128)(2,1)}, bf16[512,3072]{1,0:T(8,128)(2,1)}, u32[]{:S(2)}, u32[]{:S(2)}) collective-permute-start(bf16[512,3072]{1,0:T(8,128)(2,1)} %pad_maximum_fusion), channel_id=1, source_target_pairs={{0,1},{1,0},{2,3},{3,2},{4,5},{5,4},{6,7},{7,6},{8,9},{9,8},{10,11... | collective-permute-start | bytes 9437192 | tf_op jit(solution)/shard_map/ppermute | solution.py:27
  166.7 35.3 %collective-permute-start.7 = (bf16[512,3072]{1,0:T(8,128)(2,1)}, bf16[512,3072]{1,0:T(8,128)(2,1)}, u32[]{:S(2)}, u32[]{:S(2)}) collective-permute-start(bf16[512,3072]{1,0:T(8,128)(2,1)} %pad_maximum_fusion.1), channel_id=1, source_target_pairs={{0,1},{1,0},{2,3},{3,2},{4,5},{5,4},{6,7},{7,6},{8,9},{9,8},{10,11... | collective-permute-start | bytes 9437192 | tf_op jit(solution)/shard_map/ppermute | solution.py:27
  171.0 57.8 %collective-permute-start.3 = (bf16[384,3072]{0,1:T(8,128)(2,1)S(1)}, bf16[384,3072]{0,1:T(8,128)(2,1)}, u32[]{:S(2)}, u32[]{:S(2)}) collective-permute-start(bf16[384,3072]{0,1:T(8,128)(2,1)S(1)} %bitcast.88), channel_id=1, source_target_pairs={{0,4},{4,0},{8,12},{12,8},{16,20},{20,16},{24,28},{28,24},{1,5},{5... | collective-permute-start | bytes 7077896 | tf_op jit(solution)/shard_map/ppermute | solution.py:27
  196.7 82.3 %collective-permute-start.2 = (bf16[3072,384]{1,0:T(8,128)(2,1)}, bf16[3072,384]{1,0:T(8,128)(2,1)S(1)}, u32[]{:S(2)}, u32[]{:S(2)}) collective-permute-start(bf16[3072,384]{1,0:T(8,128)(2,1)} %bitcast.92), channel_id=1, source_target_pairs={{0,4},{4,0},{8,12},{12,8},{16,20},{20,16},{24,28},{28,24},{1,5},{5... | collective-permute-start | bytes 7077896 | tf_op jit(solution)/shard_map/ppermute | solution.py:27
  202.0 33.0 %slice-start.11 = ((s8[6291456]{0:T(1024)(128)(4,1)}), s8[4194304]{0:T(1024)(128)(4,1)S(1)}, s32[]{:S(2)}) async-start(s8[6291456]{0:T(1024)(128)(4,1)} %bitcast.119), calls=%async_computation.21 | async-start | bytes 8388608
  206.0 29.0 %slice-start.12 = ((s8[6291456]{0:T(1024)(128)(4,1)}), s8[2097152]{0:T(1024)(128)(4,1)S(1)}, s32[]{:S(2)}) async-start(s8[6291456]{0:T(1024)(128)(4,1)} %bitcast.119), calls=%async_computation.22 | async-start | bytes 4194304
  211.7 23.4 %copy-start = (bf16[8,384,384]{2,1,0:T(8,128)(2,1)S(1)}, bf16[8,384,384]{2,1,0:T(8,128)(2,1)}, u32[]{:S(2)}) copy-start(bf16[8,384,384]{2,1,0:T(8,128)(2,1)} %copy.24) | copy-start | bytes 7077892
  239.4 67.9 %copy-start.9 = (bf16[1024,384]{1,0:T(8,128)(2,1)}, bf16[1024,384]{1,0:T(8,128)(2,1)S(1)}, u32[]{:S(2)}) copy-start(bf16[1024,384]{1,0:T(8,128)(2,1)S(1)} %get-tuple-element.11) | copy-start | bytes 2359300
  279.0 12.9 %copy-start.2 = (bf16[3072,384]{1,0:T(8,128)(2,1)}, bf16[3072,384]{1,0:T(8,128)(2,1)S(1)}, u32[]{:S(2)}) copy-start(bf16[3072,384]{1,0:T(8,128)(2,1)S(1)} %collective-permute-done.2) | copy-start | bytes 7077892
  283.4 8.5 %copy-start.14 = (bf16[1024,384]{1,0:T(8,128)(2,1)}, bf16[1024,384]{1,0:T(8,128)(2,1)S(1)}, u32[]{:S(2)}) copy-start(bf16[1024,384]{1,0:T(8,128)(2,1)S(1)} %get-tuple-element.8) | copy-start | bytes 2359300
  283.4 13.9 %copy-start.12 = (bf16[1024,384]{1,0:T(8,128)(2,1)}, bf16[1024,384]{1,0:T(8,128)(2,1)S(1)}, u32[]{:S(2)}) copy-start(bf16[1024,384]{1,0:T(8,128)(2,1)S(1)} %get-tuple-element.9) | copy-start | bytes 2359300
  287.6 53.5 %collective-permute-start.10 = (bf16[3072,384]{1,0:T(8,128)(2,1)S(1)}, bf16[3072,384]{1,0:T(8,128)(2,1)S(1)}, u32[]{:S(2)}, u32[]{:S(2)}) collective-permute-start(bf16[3072,384]{1,0:T(8,128)(2,1)S(1)} %convolution_convert_fusion.1), channel_id=1, source_target_pairs={{0,4},{4,0},{8,12},{12,8},{16,20},{20,16},{24,28},{28,24},{1,5},{5... | collective-permute-start | bytes 7077896 | tf_op jit(solution)/shard_map/ppermute | solution.py:27
  295.4 63.8 %collective-permute-start.8 = (bf16[512,3072]{1,0:T(8,128)(2,1)}, bf16[512,3072]{1,0:T(8,128)(2,1)}, u32[]{:S(2)}, u32[]{:S(2)}) collective-permute-start(bf16[512,3072]{1,0:T(8,128)(2,1)} %add_convert_fusion), channel_id=1, source_target_pairs={{0,1},{1,0},{2,3},{3,2},{4,5},{5,4},{6,7},{7,6},{8,9},{9,8},{10,11... | collective-permute-start | bytes 9437192 | tf_op jit(solution)/shard_map/ppermute | solution.py:27
  302.5 73.4 %collective-permute-start.4 = (bf16[512,3072]{1,0:T(8,128)(2,1)}, bf16[512,3072]{1,0:T(8,128)(2,1)}, u32[]{:S(2)}, u32[]{:S(2)}) collective-permute-start(bf16[512,3072]{1,0:T(8,128)(2,1)} %add_convert_fusion.1), channel_id=1, source_target_pairs={{0,1},{1,0},{2,3},{3,2},{4,5},{5,4},{6,7},{7,6},{8,9},{9,8},{10,11... | collective-permute-start | bytes 9437192 | tf_op jit(solution)/shard_map/ppermute | solution.py:27
  345.9 6.9 %copy-start.15 = (bf16[1024,384]{1,0:T(8,128)(2,1)S(1)}, bf16[1024,384]{1,0:T(8,128)(2,1)}, u32[]{:S(2)}) copy-start(bf16[1024,384]{1,0:T(8,128)(2,1)} %copy-done.14) | copy-start | bytes 2359300
  345.9 13.3 %slice-start.2 = ((s8[6291456]{0:T(1024)(128)(4,1)}), s8[2097152]{0:T(1024)(128)(4,1)S(1)}, s32[]{:S(2)}) async-start(s8[6291456]{0:T(1024)(128)(4,1)} %bitcast.86), calls=%async_computation.12 | async-start | bytes 4194304
  345.9 66.3 %all-to-all-start.4 = ((bf16[8,384,384]{2,1,0:T(8,128)(2,1)}), bf16[8,384,384]{2,1,0:T(8,128)(2,1)}, u32[]{:S(2)}, u32[]{:S(2)}) async-start(bf16[8,384,384]{2,1,0:T(8,128)(2,1)} %bitcast.118), calls=%async_computation.4 | async-start | bytes 4718592 | tf_op jit(solution)/shard_map/all_to_all | solution.py:131
  352.8 6.4 %slice-start.3 = ((s8[6291456]{0:T(1024)(128)(4,1)}), s8[4194304]{0:T(1024)(128)(4,1)S(1)}, s32[]{:S(2)}) async-start(s8[6291456]{0:T(1024)(128)(4,1)} %bitcast.86), calls=%async_computation.13 | async-start | bytes 8388608
  367.3 8.5 %slice-start = ((s8[6291456]{0:T(1024)(128)(4,1)}), s8[4194304]{0:T(1024)(128)(4,1)S(1)}, s32[]{:S(2)}) async-start(s8[6291456]{0:T(1024)(128)(4,1)} %bitcast.84), calls=%async_computation.10 | async-start | bytes 8388608
  370.7 5.1 slice-start.1
  370.8 37.6 %collective-permute-start.9 = (bf16[256,3072]{1,0:T(8,128)(2,1)}, bf16[256,3072]{1,0:T(8,128)(2,1)}, u32[]{:S(2)}, u32[]{:S(2)}) collective-permute-start(bf16[256,3072]{1,0:T(8,128)(2,1)} %slice.154), channel_id=1, source_target_pairs={{0,2},{1,3},{2,0},{3,1},{4,6},{5,7},{6,4},{7,5},{8,10},{9,11},{10,... | collective-permute-start | bytes 4718600 | tf_op jit(solution)/shard_map/ppermute | solution.py:27
  385.9 53.6 %collective-permute-start.5 = (bf16[256,3072]{1,0:T(8,128)(2,1)}, bf16[256,3072]{1,0:T(8,128)(2,1)}, u32[]{:S(2)}, u32[]{:S(2)}) collective-permute-start(bf16[256,3072]{1,0:T(8,128)(2,1)} %slice.155), channel_id=1, source_target_pairs={{0,2},{1,3},{2,0},{3,1},{4,6},{5,7},{6,4},{7,5},{8,10},{9,11},{10,... | collective-permute-start | bytes 4718600 | tf_op jit(solution)/shard_map/ppermute | solution.py:27
  412.3 5.4 copy-start.13
  412.3 27.3 %slice-start.4 = ((s8[6291456]{0:T(1024)(128)(4,1)}), s8[2097152]{0:T(1024)(128)(4,1)S(1)}, s32[]{:S(2)}) async-start(s8[6291456]{0:T(1024)(128)(4,1)} %bitcast.96), calls=%async_computation.14 | async-start | bytes 4194304
  412.3 37.3 %all-to-all-start.3 = ((bf16[4,64,3072]{2,1,0:T(8,128)(2,1)}), bf16[4,64,3072]{2,1,0:T(8,128)(2,1)}, u32[]{:S(2)}, u32[]{:S(2)}) async-start(bf16[4,64,3072]{2,1,0:T(8,128)(2,1)} %bitcast.106), calls=%async_computation.3 | async-start | bytes 3145728 | tf_op jit(solution)/shard_map/all_to_all | solution.py:101
  417.6 22.0 %slice-start.5 = ((s8[6291456]{0:T(1024)(128)(4,1)}), s8[4194304]{0:T(1024)(128)(4,1)S(1)}, s32[]{:S(2)}) async-start(s8[6291456]{0:T(1024)(128)(4,1)} %bitcast.96), calls=%async_computation.15 | async-start | bytes 8388608
  424.6 47.9 %collective-permute-start.11 = (bf16[384,3072]{1,0:T(8,128)(2,1)}, bf16[384,3072]{1,0:T(8,128)(2,1)}, u32[]{:S(2)}, u32[]{:S(2)}) collective-permute-start(bf16[384,3072]{1,0:T(8,128)(2,1)} %convolution_convert_fusion), channel_id=1, source_target_pairs={{0,4},{4,0},{8,12},{12,8},{16,20},{20,16},{24,28},{28,24},{1,5},{5... | collective-permute-start | bytes 7077896 | tf_op jit(solution)/shard_map/ppermute | solution.py:27
  442.6 30.0 %copy-start.10 = (bf16[1024,384]{1,0:T(8,128)(2,1)S(1)}, bf16[1024,384]{1,0:T(8,128)(2,1)}, u32[]{:S(2)}) copy-start(bf16[1024,384]{1,0:T(8,128)(2,1)} %copy-done.9) | copy-start | bytes 2359300
  449.6 38.9 %all-to-all-start.2 = ((bf16[4,64,3072]{2,1,0:T(8,128)(2,1)}), bf16[4,64,3072]{2,1,0:T(8,128)(2,1)S(1)}, u32[]{:S(2)}, u32[]{:S(2)}) async-start(bf16[4,64,3072]{2,1,0:T(8,128)(2,1)} %bitcast.107), calls=%async_computation.2 | async-start | bytes 3145728 | tf_op jit(solution)/shard_map/all_to_all | solution.py:101
  489.6 57.0 %all-to-all-start.5 = ((bf16[8,384,384]{2,1,0:T(8,128)(2,1)}), bf16[8,384,384]{2,1,0:T(8,128)(2,1)S(1)}, u32[]{:S(2)}, u32[]{:S(2)}) async-start(bf16[8,384,384]{2,1,0:T(8,128)(2,1)} %bitcast.103), calls=%async_computation.5 | async-start | bytes 4718592 | tf_op jit(solution)/shard_map/all_to_all | solution.py:137
  493.3 96.7 %all-gather.8.cloned.1.call-start = ((), (), s32[]{:S(2)}) async-start(), calls=%async_computation.7 | async-start | bytes 1966080 | tf_op jit(solution)/shard_map/all_gather | solution.py:154
  498.1 94.5 %all-gather.12.cloned.1.call-start = ((), (), s32[]{:S(2)}) async-start(), calls=%async_computation.9 | async-start | bytes 1966080 | tf_op jit(solution)/shard_map/all_gather | solution.py:154
  503.1 46.2 %copy-start.24 = (f32[64]{0:T(128)S(1)}, f32[64]{0:T(128)}, u32[]{:S(2)}) copy-start(f32[64]{0:T(128)} %copy-done.22) | copy-start | bytes 772
  503.1 46.2 %copy-start.26 = (f32[64]{0:T(128)S(1)}, f32[64]{0:T(128)}, u32[]{:S(2)}) copy-start(f32[64]{0:T(128)} %copy-done.25) | copy-start | bytes 772
  503.1 46.2 %copy-start.28 = (f32[64]{0:T(128)S(1)}, f32[64]{0:T(128)}, u32[]{:S(2)}) copy-start(f32[64]{0:T(128)} %copy-done.27) | copy-start | bytes 772
  (16 other events, 24.7 us)
Sparse Core Ops, SparseCore 0:
  13.6 77.7 all-gather.5
  93.6 34.2 all-gather.9
  498.2 20.9 all-gather.7
  520.7 19.6 all-gather.11
